TPU v7x, 32 devices: a whole 2x2x4 slice. The times are simulated.
32 devices in a mesh: grp: 2 (over y), gy: 4 (over z), gx: 2 (over x), gz: 2 (over core).
Axes of the slice: x: 2, y: 2, z: 4, core: 2. Of those that a mesh axis runs over, the one named last changes fastest.
Arguments:
- pair: bfloat16 [1024, 512, 128], P(('grp', 'gx', 'gz'), 'gy'), parts along dimension 0, may hold values from -6 to 6
- lengths: int32 [2], P('grp'), parts along dimension 0, may hold values from 256 to 512
- ln_gain: float32 [128], replicated, may hold values from 0.1 to 1.9
- ln_bias: float32 [128], replicated, may hold values from -3 to 3
- w_ab: bfloat16 [128, 512], replicated, may hold values from -0.5 to 0.5
- w_gate: bfloat16 [128, 128], replicated, may hold values from -0.5 to 0.5
- out_gain: float32 [128], replicated, may hold values from 0.1 to 1.9
- out_bias: float32 [128], replicated, may hold values from -3 to 3
- w_out: bfloat16 [128, 128], replicated, may hold values from -0.5 to 0.5
Outputs:
- update: bfloat16 [1024, 512, 128], P(('grp', 'gx', 'gz'), 'gy'), parts along dimension 0
There are 2 independent parts, one for each index of `grp`. A program takes and returns all parts, laid end to end along the dimension named above; an argument that names none is the same for every part. Nothing has to cross between parts.
Inputs may be any that keep to these rules, and one draw needn't show every extreme that they name: Residues from lengths[0] on are padding.
All inputs are finite; a program needn't handle non-finite values.
Results may differ from a plain program's by a relative error of at most 0.0052.
Values may be sent and summed in bfloat16 or wider, within the bound.
A program may use at most 128 MiB of HBM per device.

v0:
```python
import jax
import jax.numpy as jnp
from jax import lax
from jax.sharding import PartitionSpec as P


def layer_norm(values, gain, bias):
    values = values.astype(jnp.float32)
    mean = jnp.mean(values, -1, keepdims=True)
    spread = jnp.mean(jnp.square(values - mean), -1, keepdims=True)
    return (values - mean) * lax.rsqrt(spread + 1e-05) * gain + bias


def channel_norm(values, gain, bias):
    mean = jnp.mean(values, 0, keepdims=True)
    spread = jnp.mean(jnp.square(values - mean), 0, keepdims=True)
    return (values - mean) * lax.rsqrt(spread + 1e-05) * gain[:, None, None] + bias[:, None, None]


def body(pair, lengths, ln_gain, ln_bias, w_ab, w_gate, out_gain, out_bias, w_out):
    tile_rows, tile_cols, width = pair.shape
    hidden = w_out.shape[0]
    row_start = lax.axis_index(("gx", "gz")) * tile_rows
    col_index = lax.axis_index("gy")
    col_start = col_index * tile_cols
    normed = layer_norm(pair, ln_gain, ln_bias).astype(jnp.bfloat16)
    flat = normed.reshape(tile_rows * tile_cols, width)
    proj = jnp.dot(flat, w_ab, preferred_element_type=jnp.float32).reshape(
        tile_rows, tile_cols, 4 * hidden
    )
    row_live = (row_start + jnp.arange(tile_rows, dtype=jnp.int32) < lengths[0]).astype(jnp.float32)
    col_live = (col_start + jnp.arange(tile_cols, dtype=jnp.int32) < lengths[0]).astype(jnp.float32)
    pair_mask = (row_live[:, None] * col_live[None, :])[..., None]
    left = (pair_mask * jax.nn.sigmoid(proj[..., :hidden]) * proj[..., hidden : 2 * hidden]).astype(
        jnp.bfloat16
    )
    right = (
        pair_mask * jax.nn.sigmoid(proj[..., 2 * hidden : 3 * hidden]) * proj[..., 3 * hidden :]
    ).astype(jnp.bfloat16)
    left_major = jnp.transpose(left, (2, 0, 1))
    right_major = jnp.transpose(right, (2, 0, 1))
    column_rows = lax.all_gather(right_major, ("gx", "gz"), axis=1, tiled=True)
    right_mine = lax.all_to_all(column_rows, "gy", split_axis=1, concat_axis=2, tiled=True)
    triangle = jnp.einsum(
        "cik,cjk->cij",
        lax.all_gather(left_major, "gy", axis=2, tiled=True),
        right_mine,
        preferred_element_type=jnp.float32,
    )
    tri_norm = channel_norm(triangle, out_gain, out_bias).astype(jnp.bfloat16)
    gate = jax.nn.sigmoid(jnp.dot(flat, w_gate, preferred_element_type=jnp.float32)).reshape(
        tile_rows, tile_cols, width
    )
    projected = jnp.einsum("cij,cd->ijd", tri_norm, w_out, preferred_element_type=jnp.float32)
    return (gate * projected).astype(jnp.bfloat16)


def solution(mesh):
    in_specs = (P(("grp", "gx", "gz"), "gy", None), P("grp"), P(), P(), P(), P(), P(), P(), P())
    out_specs = P(("grp", "gx", "gz"), "gy", None)
    return jax.shard_map(body, mesh=mesh, in_specs=in_specs, out_specs=out_specs, check_vma=False)
```

profile of v0, /device:TPU:0, one launch (start us, length us, event | category | flops | bytes accessed | tf_op | source)
XLA Modules:
  0.0 898.8 jit_solution(9406988459465322010)
XLA Ops:
  6.5 0.0 copy-start
  6.5 0.0 copy-start.7
  6.5 0.0 copy-start.6
  6.5 0.0 all-gather.5.cloned.1.call-start
  6.6 0.0 copy-start.3
  7.4 3.8 convert_reduce_fusion
  11.2 6.0 fusion.5
  17.2 0.1 broadcast_multiply_fusion
  17.3 0.0 copy-done.7
  17.3 0.0 copy-done.6
  17.3 0.0 copy-done.3
  17.4 4.9 fusion.8
  22.3 0.0 copy-done
  22.3 0.0 copy-start.4
  22.3 13.1 %fusion.25 = f32[128,128,512]{2,1,0:T(8,128)} fusion(bf16[128,128,128]{2,1,0:T(8,128)(2,1)S(1)} %fusion.8, bf16[128,512]{1,0:T(8,128)(2,1)S(1)} %copy-done), kind=kOutput, calls=%fused_computation.34 | convolution fusion | flops 2147483648 | bytes 37879808 | tf_op jit(solution)/shard_map/dot_general | solution.py:28
  35.5 0.0 copy-done.4
  35.5 15.6 %fusion.22 = (bf16[128,128,128]{0,2,1:T(8,128)(2,1)}, bf16[128,128,128]{0,2,1:T(8,128)(2,1)}) fusion(f32[128,128,512]{2,1,0:T(8,128)} %fusion.25, f32[128,128]{1,0:T(8,128)S(1)} %broadcast_multiply_fusion), kind=kLoop, calls=%fused_computation.33 | loop fusion | flops 25165824 | bytes 42008576 | tf_op jit(solution)/shard_map/transpose | solution.py:41
  51.1 6.4 copy.13
  57.4 0.0 all-gather.5.cloned.1.call-update
  57.5 0.0 all-gather.3.cloned.1.call-start
  57.5 0.7 all-gather.3.cloned.1.call-update
  58.2 0.0 copy-start.10
  58.2 108.0 %all-gather.5.cloned.1.call-done = bf16[128,512,128]{2,0,1:T(8,128)(2,1)} async-done(((bf16[128,128,128]{2,0,1:T(8,128)(2,1)}), bf16[128,512,128]{2,0,1:T(8,128)(2,1)}) %all-gather.5.cloned.1.call-update) | async-done | bytes 16777232 | tf_op jit(solution)/shard_map/all_gather | solution.py:42
  166.2 7.3 all-to-all-start
  173.5 0.0 copy-done.10
  173.5 9.0 %fusion.2 = f32[16384,128]{1,0:T(8,128)} fusion(bf16[16384,128]{1,0:T(8,128)(2,1)} %bitcast.24, bf16[128,128]{1,0:T(8,128)(2,1)S(1)} %copy-done.10), kind=kOutput, calls=%fused_computation.3 | convolution fusion | flops 543162368 | bytes 12615680 | tf_op jit(solution)/shard_map/dot_general | solution.py:51
  182.5 580.3 %all-gather.3.cloned.1.call-done = bf16[128,128,512]{0,2,1:T(8,128)(2,1)} async-done(((bf16[128,128,128]{0,2,1:T(8,128)(2,1)}), bf16[128,128,512]{0,2,1:T(8,128)(2,1)}) %all-gather.3.cloned.1.call-update) | async-done | bytes 16777232 | tf_op jit(solution)/shard_map/all_gather | solution.py:46
  762.8 23.4 %copy.15 = bf16[128,128,512]{2,1,0:T(8,128)(2,1)} copy(bf16[128,128,512]{0,2,1:T(8,128)(2,1)} %all-gather.3.cloned.1.call-done) | data formatting | bytes 33554432 | tf_op jit(solution)/shard_map/all_gather | solution.py:46
  786.2 20.3 %all-to-all-done = bf16[128,512,128]{2,0,1:T(8,128)(2,1)} async-done(((bf16[128,512,128]{2,0,1:T(8,128)(2,1)}), bf16[128,512,128]{2,0,1:T(8,128)(2,1)}, u32[]{:S(2)}, u32[]{:S(2)}) %all-to-all-start) | async-done | bytes 16777248 | tf_op jit(solution)/shard_map/all_to_all | solution.py:43
  806.5 22.0 %copy.22 = bf16[128,4,128,128]{3,1,2,0:T(4,128)(2,1)} copy(bf16[128,4,128,128]{3,0,2,1:T(8,128)(2,1)} %bitcast.6) | data formatting | bytes 33554432 | tf_op jit(solution)/shard_map/all_to_all | solution.py:43
  828.6 24.9 %all_to_all.16 = bf16[128,128,512]{2,1,0:T(8,128)(2,1)} reshape(bf16[128,128,4,128]{3,2,1,0:T(4,128)(2,1)} %bitcast.23) | data formatting | bytes 33554432 | tf_op jit(solution)/shard_map/all_to_all | solution.py:43
  853.4 16.4 %fusion.28 = (f32[128,128]{1,0:T(8,128)S(1)}, f32[128,128,128]{2,1,0:T(8,128)}) fusion(bf16[128,128,512]{2,1,0:T(8,128)(2,1)} %copy.15, bf16[128,128,512]{2,1,0:T(8,128)(2,1)} %all_to_all.16), kind=kOutput, calls=%fused_computation.44 | convolution fusion | flops 2149564416 | bytes 42008576 | tf_op jit(solution)/shard_map/cik,cjk->cij/dot_general | solution.py:44
  869.8 0.0 copy-start.2
  869.8 0.0 copy-start.8
  869.8 0.0 copy-start.9
  869.8 4.4 multiply_reduce_fusion
  874.2 0.0 copy-start.5
  874.3 1.3 copy-done.2
  875.6 0.0 copy-done.8
  875.6 0.0 copy-done.9
  875.6 2.0 add_convert_fusion
  877.6 0.0 copy-start.1
  877.6 0.0 copy-done.5
  877.6 14.4 %multiply_convert_fusion = bf16[128,128,128]{2,1,0:T(8,128)(2,1)} fusion(f32[128,128,128]{2,1,0:T(8,128)} %bitcast.25, bf16[128,128,128]{2,1,0:T(8,128)(2,1)S(1)} %add_convert_fusion, bf16[128,128]{1,0:T(8,128)(2,1)S(1)} %copy-done.5), kind=kOutput, calls=%fused_computation.27 | convolution fusion | flops 541065216 | bytes 16809984 | tf_op jit(solution)/shard_map/cij,cd->ijd/dot_general | solution.py:54
  891.9 0.0 copy-done.1
  (5 shorter events, 0.1 us)
Async XLA Ops:
  6.5 15.8 %copy-start = (bf16[128,512]{1,0:T(8,128)(2,1)S(1)}, bf16[128,512]{1,0:T(8,128)(2,1)}, u32[]{:S(2)}) copy-start(bf16[128,512]{1,0:T(8,128)(2,1)} %param.13) | copy-start | bytes 393220
  6.5 10.8 %copy-start.7 = (f32[128]{0:T(128)S(1)}, f32[128]{0:T(128)}, u32[]{:S(2)}) copy-start(f32[128]{0:T(128)} %param.11) | copy-start | bytes 1540
  6.5 10.8 %copy-start.6 = (f32[128]{0:T(128)S(1)}, f32[128]{0:T(128)}, u32[]{:S(2)}) copy-start(f32[128]{0:T(128)} %param.12) | copy-start | bytes 1540
  6.5 159.7 %all-gather.5.cloned.1.call-start = ((), (), s32[]{:S(2)}) async-start(), calls=%async_computation.2 | async-start | bytes 20971520 | tf_op jit(solution)/shard_map/all_gather | solution.py:42
  6.6 10.8 %copy-start.3 = (bf16[128,128,128]{2,1,0:T(8,128)(2,1)S(1)}, bf16[128,128,128]{2,1,0:T(8,128)(2,1)}, u32[]{:S(2)}) copy-start(bf16[128,128,128]{2,1,0:T(8,128)(2,1)} %param.9) | copy-start | bytes 12582916
  22.3 13.2 %copy-start.4 = (bf16[128,128,128]{2,1,0:T(8,128)(2,1)}, bf16[128,128,128]{2,1,0:T(8,128)(2,1)S(1)}, u32[]{:S(2)}) copy-start(bf16[128,128,128]{2,1,0:T(8,128)(2,1)S(1)} %fusion.8) | copy-start | bytes 12582916
  57.5 705.3 %all-gather.3.cloned.1.call-start = ((), (), s32[]{:S(2)}) async-start(), calls=%async_computation.1 | async-start | bytes 20971520 | tf_op jit(solution)/shard_map/all_gather | solution.py:46
  58.2 115.3 %copy-start.10 = (bf16[128,128]{1,0:T(8,128)(2,1)S(1)}, bf16[128,128]{1,0:T(8,128)(2,1)}, u32[]{:S(2)}) copy-start(bf16[128,128]{1,0:T(8,128)(2,1)} %param.14) | copy-start | bytes 98308
  166.2 640.3 %all-to-all-start = ((bf16[128,512,128]{2,0,1:T(8,128)(2,1)}), bf16[128,512,128]{2,0,1:T(8,128)(2,1)}, u32[]{:S(2)}, u32[]{:S(2)}) async-start(bf16[128,512,128]{2,0,1:T(8,128)(2,1)} %all-gather.5.cloned.1.call-done), calls=%async_computation | async-start | bytes 33554432 | tf_op jit(solution)/shard_map/all_to_all | solution.py:43
  869.8 5.8 copy-start.2
  869.8 5.8 copy-start.8
  869.8 5.8 copy-start.9
  874.2 3.3 copy-start.5
  877.6 14.4 %copy-start.1 = (bf16[128,512]{1,0:T(8,128)(2,1)S(1)}, bf16[128,512]{1,0:T(8,128)(2,1)}, u32[]{:S(2)}) copy-start(bf16[128,512]{1,0:T(8,128)(2,1)} %param.13) | copy-start | bytes 393220
Sparse Core Ops, SparseCore 0:
  57.6 108.6 all-gather.4
  167.8 594.9 all-gather.2
where the time goes:
time: 900 us; the launch traced here: 899 us
  waiting for transfers between devices  709 us (79%)
  local copies, waits for them, and re-layouts  78 us (9%)
  matrix products  52.9 us (6%)
  other arithmetic  36.9 us (4%)
  between operations  14.4 us (2%)
    all_gather x1, waiting for transfers between devices, body(): lax.all_gather(left_major, 'gy', axis=2, tiled=True)  580 us
    all_gather x1, waiting for transfers between devices, body(): column_rows = lax.all_gather(right_major, ('gx', 'gz'), axis=1, tiled=True)  108 us
    all_to_all x2, local copies, waits for them, and re-layouts, body(): lax.all_to_all(column_rows, 'gy', split_axis=1, concat_axis=2, tiled=True)  46.9 us
    all_gather x1, local copies, waits for them, and re-layouts, body(): lax.all_gather(left_major, 'gy', axis=2, tiled=True)  23.4 us
    all_to_all x1, waiting for transfers between devices, body(): lax.all_to_all(column_rows, 'gy', split_axis=1, concat_axis=2, tiled=True)  20.3 us
  transfers between devices with their start and end apart: 3, of which 3 were waited for; matrix products, arithmetic and copies ran while one was open for 4% of the time, Pallas kernels for 0%

commit v1 on v0

--- a/solution.py
+++ b/solution.py
@@ -2,6 +2,18 @@
 import jax.numpy as jnp
 from jax import lax
 from jax.sharding import PartitionSpec as P
+
+
+def summed_around(x, axis, dim, contribution):
+    peers, index = (lax.axis_size(axis), lax.axis_index(axis))
+    downward = [(i, (i - 1) % peers) for i in range(peers)]
+    extent = x.shape[dim]
+    held = x
+    total = contribution(held, index * extent)
+    for hop in range(1, peers):
+        held = lax.ppermute(held, axis, downward)
+        total = total + contribution(held, (index + hop) % peers * extent)
+    return total
 
 
 def layer_norm(values, gain, bias):
@@ -41,11 +53,16 @@
     right_major = jnp.transpose(right, (2, 0, 1))
     column_rows = lax.all_gather(right_major, ("gx", "gz"), axis=1, tiled=True)
     right_mine = lax.all_to_all(column_rows, "gy", split_axis=1, concat_axis=2, tiled=True)
-    triangle = jnp.einsum(
-        "cik,cjk->cij",
-        lax.all_gather(left_major, "gy", axis=2, tiled=True),
-        right_mine,
-        preferred_element_type=jnp.float32,
+    triangle = summed_around(
+        left_major,
+        "gy",
+        2,
+        lambda own_block, at: jnp.einsum(
+            "cik,cjk->cij",
+            own_block,
+            lax.dynamic_slice_in_dim(right_mine, at, own_block.shape[2], axis=2),
+            preferred_element_type=jnp.float32,
+        ),
     )
     tri_norm = channel_norm(triangle, out_gain, out_bias).astype(jnp.bfloat16)
     gate = jax.nn.sigmoid(jnp.dot(flat, w_gate, preferred_element_type=jnp.float32)).reshape(

time: 900 us -> 937 us (1.041)
  matrix products: 52.9 us -> 77.1 us
    ppermute x0 -> x3, waiting for transfers between devices: none -> 600 us  [summed_around(): held = lax.ppermute(held, axis, downward)]
    all_gather x1 -> x0, waiting for transfers between devices: 580 us -> none  [body(): lax.all_gather(left_major, 'gy', axis=2, tiled=True)]
    dot_general x1 -> x4, matrix products: 16.4 us -> 41.9 us  [body(): jnp.einsum('cik,cjk->cij', own_block, lax.dynamic_slice_in_dim(right_mine...]
    all_gather x1 -> x0, local copies, waits for them, and re-layouts: 23.4 us -> none  [body(): lax.all_gather(left_major, 'gy', axis=2, tiled=True)]
    all_to_all x1, waiting for transfers between devices: 20.3 us -> 0.01 us  [body(): lax.all_to_all(column_rows, 'gy', split_axis=1, concat_axis=2, tiled=True)]
    ppermute x0 -> x3, local copies, waits for them, and re-layouts: none -> 20.2 us  [summed_around(): held = lax.ppermute(held, axis, downward)]
  transfers between devices with their start and end apart: 3 -> 5, of which waited for: 3 -> 4; matrix products, arithmetic and copies ran while one was open for 4% -> 4% of each run, Pallas kernels for 0% -> 0%
where the time goes in v1:
time: 937 us; the launch traced here: 935 us
  waiting for transfers between devices  709 us (76%)
  local copies, waits for them, and re-layouts  83.5 us (9%)
  matrix products  77.1 us (8%)
  other arithmetic  36.7 us (4%)
  starting transfers between devices  15 us (2%)
  between operations  14.4 us (2%)
    ppermute x3, waiting for transfers between devices, summed_around(): held = lax.ppermute(held, axis, downward)  600 us
    all_gather x1, waiting for transfers between devices, body(): column_rows = lax.all_gather(right_major, ('gx', 'gz'), axis=1, tiled=True)  109 us
    all_to_all x2, local copies, waits for them, and re-layouts, body(): lax.all_to_all(column_rows, 'gy', split_axis=1, concat_axis=2, tiled=True)  46.9 us
    dot_general x4, matrix products, body(): jnp.einsum('cik,cjk->cij', own_block, lax.dynamic_slice_in_dim(right_mine...  41.9 us
    ppermute x3, local copies, waits for them, and re-layouts, summed_around(): held = lax.ppermute(held, axis, downward)  20.2 us
  transfers between devices with their start and end apart: 5, of which 4 were waited for; matrix products, arithmetic and copies ran while one was open for 4% of the time, Pallas kernels for 0%

profile of v1, /device:TPU:0, one launch (start us, length us, event | category | flops | bytes accessed | tf_op | source)
XLA Modules:
  0.0 935.2 jit_solution(15680076525316108245)
XLA Ops:
  6.5 0.0 copy-start
  6.5 0.0 copy-start.10
  6.5 0.0 copy-start.9
  6.5 0.0 all-gather.2.cloned.1.call-start
  6.6 0.0 copy-start.4
  7.4 3.8 convert_reduce_fusion
  11.2 6.0 fusion.5
  17.2 0.1 broadcast_multiply_fusion
  17.3 0.0 copy-done.10
  17.3 0.0 copy-done.9
  17.4 0.0 copy-done.4
  17.4 4.9 fusion.8
  22.3 0.0 copy-done
  22.3 0.0 copy-start.5
  22.3 13.1 %fusion.35 = f32[128,128,512]{2,1,0:T(8,128)} fusion(bf16[128,128,128]{2,1,0:T(8,128)(2,1)S(1)} %fusion.8, bf16[128,512]{1,0:T(8,128)(2,1)S(1)} %copy-done), kind=kOutput, calls=%fused_computation.43 | convolution fusion | flops 2147483648 | bytes 37879808 | tf_op jit(solution)/shard_map/dot_general | solution.py:40
  35.4 0.0 copy-done.5
  35.4 15.4 %fusion.30 = (bf16[128,128,128]{0,2,1:T(8,128)(2,1)}, bf16[128,128,128]{0,2,1:T(8,128)(2,1)}) fusion(f32[128,128,512]{2,1,0:T(8,128)} %fusion.35, f32[128,128]{1,0:T(8,128)S(1)} %broadcast_multiply_fusion), kind=kLoop, calls=%fused_computation.42 | loop fusion | flops 25165824 | bytes 42008576 | tf_op jit(solution)/shard_map/transpose | solution.py:53
  50.8 6.4 copy.16
  57.2 0.0 all-gather.2.cloned.1.call-update
  57.2 108.8 %all-gather.2.cloned.1.call-done = bf16[128,512,128]{2,0,1:T(8,128)(2,1)} async-done(((bf16[128,128,128]{2,0,1:T(8,128)(2,1)}), bf16[128,512,128]{2,0,1:T(8,128)(2,1)}) %all-gather.2.cloned.1.call-update) | async-done | bytes 16777232 | tf_op jit(solution)/shard_map/all_gather | solution.py:54
  166.0 7.0 all-to-all-start
  173.0 0.0 copy-start.13
  173.0 3.8 collective-permute-start
  176.8 356.7 %collective-permute-done = bf16[128,128,128]{0,2,1:T(8,128)(2,1)S(1)} collective-permute-done((bf16[128,128,128]{0,2,1:T(8,128)(2,1)}, bf16[128,128,128]{0,2,1:T(8,128)(2,1)S(1)}, u32[]{:S(2)}, u32[]{:S(2)}) %collective-permute-start) | collective-permute-done | bytes 4194336 | tf_op jit(solution)/shard_map/ppermute | solution.py:14
  533.5 0.0 copy-start.7
  533.5 2.0 copy-done.7
  535.5 4.2 collective-permute-start.1
  539.7 179.4 %collective-permute-done.1 = bf16[128,128,128]{0,2,1:T(8,128)(2,1)} collective-permute-done((bf16[128,128,128]{0,2,1:T(8,128)(2,1)S(1)}, bf16[128,128,128]{0,2,1:T(8,128)(2,1)}, u32[]{:S(2)}, u32[]{:S(2)}) %collective-permute-start.1) | collective-permute-done | bytes 4194336 | tf_op jit(solution)/shard_map/ppermute | solution.py:14
  719.1 0.0 collective-permute-start.2
  719.1 6.7 copy.18
  725.8 0.0 copy-done.13
  725.8 7.8 fusion.2
  733.5 6.7 copy.19
  740.3 6.7 copy.20
  747.0 63.7 %collective-permute-done.2 = bf16[128,128,128]{0,2,1:T(8,128)(2,1)} collective-permute-done((bf16[128,128,128]{0,2,1:T(8,128)(2,1)}, bf16[128,128,128]{0,2,1:T(8,128)(2,1)}, u32[]{:S(2)}, u32[]{:S(2)}) %collective-permute-start.2) | collective-permute-done | bytes 4194336 | tf_op jit(solution)/shard_map/ppermute | solution.py:14
  810.7 6.7 copy.21
  817.4 0.0 all-to-all-done
  817.4 22.0 %copy.28 = bf16[128,4,128,128]{3,1,2,0:T(4,128)(2,1)} copy(bf16[128,4,128,128]{3,0,2,1:T(8,128)(2,1)} %bitcast.6) | data formatting | bytes 33554432 | tf_op jit(solution)/shard_map/all_to_all | solution.py:55
  839.4 24.9 %all_to_all.16 = bf16[128,128,512]{2,1,0:T(8,128)(2,1)} reshape(bf16[128,128,4,128]{3,2,1,0:T(4,128)(2,1)} %bitcast.25) | data formatting | bytes 33554432 | tf_op jit(solution)/shard_map/all_to_all | solution.py:55
  864.3 0.0 copy-start.3
  864.3 10.1 %fusion.25 = f32[128,128,128]{2,1,0:T(8,128)} fusion(bf16[128,128,128]{2,1,0:T(8,128)(2,1)} %copy.19, bf16[128,128,512]{2,1,0:T(8,128)(2,1)} %all_to_all.16, s32[]{:T(128)S(6)} %select_n.29), kind=kOutput, calls=%fused_computation.37 | convolution fusion | flops 536870912 | bytes 16777220 | tf_op jit(solution)/shard_map/cik,cjk->cij/dot_general | solution.py:60
  874.5 0.0 copy-done.3
  874.5 0.0 copy-start.6
  874.5 8.6 fusion.23
  883.1 0.0 copy-done.6
  883.1 6.2 fusion.27
  889.4 16.9 %fusion.42 = (f32[128,128]{1,0:T(8,128)S(1)}, f32[128,128,128]{2,1,0:T(8,128)}) fusion(bf16[128,128,128]{2,1,0:T(8,128)(2,1)} %copy.21, bf16[128,128,512]{2,1,0:T(8,128)(2,1)} %all_to_all.16, s32[]{:T(128)S(6)} %select_n.33, f32[128,128,128]{2,1,0:T(8,128)} %fusion.23, f32[128,128,128]{2,1,0:T(8,128)} %fusion.27, f32[128,128,128]{2,1,0:T(8,128)} %fusion.25), kind=kOutput, calls=%fused_computation.57 | convolution fusion | flops 545243136 | bytes 42008580 | tf_op jit(solution)/shard_map/cik,cjk->cij/dot_general | solution.py:60
  906.2 0.0 copy-start.2
  906.2 0.0 copy-start.11
  906.2 0.0 copy-start.12
  906.2 4.4 multiply_reduce_fusion
  910.7 0.0 copy-start.8
  910.7 1.3 copy-done.2
  912.0 0.0 copy-done.11
  912.0 0.0 copy-done.12
  912.0 2.0 add_convert_fusion
  914.0 0.0 copy-start.1
  914.0 0.0 copy-done.8
  914.0 14.4 %multiply_convert_fusion = bf16[128,128,128]{2,1,0:T(8,128)(2,1)} fusion(f32[128,128,128]{2,1,0:T(8,128)} %bitcast.27, bf16[128,128,128]{2,1,0:T(8,128)(2,1)S(1)} %add_convert_fusion, bf16[128,128]{1,0:T(8,128)(2,1)S(1)} %copy-done.8), kind=kOutput, calls=%fused_computation.27 | convolution fusion | flops 541065216 | bytes 16809984 | tf_op jit(solution)/shard_map/cij,cd->ijd/dot_general | solution.py:71
  928.4 0.0 copy-done.1
  (5 shorter events, 0.1 us)
Async XLA Ops:
  6.5 15.8 %copy-start = (bf16[128,512]{1,0:T(8,128)(2,1)S(1)}, bf16[128,512]{1,0:T(8,128)(2,1)}, u32[]{:S(2)}) copy-start(bf16[128,512]{1,0:T(8,128)(2,1)} %param.13) | copy-start | bytes 393220
  6.5 10.8 %copy-start.10 = (f32[128]{0:T(128)S(1)}, f32[128]{0:T(128)}, u32[]{:S(2)}) copy-start(f32[128]{0:T(128)} %param.11) | copy-start | bytes 1540
  6.5 10.8 %copy-start.9 = (f32[128]{0:T(128)S(1)}, f32[128]{0:T(128)}, u32[]{:S(2)}) copy-start(f32[128]{0:T(128)} %param.12) | copy-start | bytes 1540
  6.5 159.5 %all-gather.2.cloned.1.call-start = ((), (), s32[]{:S(2)}) async-start(), calls=%async_computation.1 | async-start | bytes 20971520 | tf_op jit(solution)/shard_map/all_gather | solution.py:54
  6.6 10.8 %copy-start.4 = (bf16[128,128,128]{2,1,0:T(8,128)(2,1)S(1)}, bf16[128,128,128]{2,1,0:T(8,128)(2,1)}, u32[]{:S(2)}) copy-start(bf16[128,128,128]{2,1,0:T(8,128)(2,1)} %param.9) | copy-start | bytes 12582916
  22.3 13.1 %copy-start.5 = (bf16[128,128,128]{2,1,0:T(8,128)(2,1)}, bf16[128,128,128]{2,1,0:T(8,128)(2,1)S(1)}, u32[]{:S(2)}) copy-start(bf16[128,128,128]{2,1,0:T(8,128)(2,1)S(1)} %fusion.8) | copy-start | bytes 12582916
  166.0 651.4 %all-to-all-start = ((bf16[128,512,128]{2,0,1:T(8,128)(2,1)}), bf16[128,512,128]{2,0,1:T(8,128)(2,1)}, u32[]{:S(2)}, u32[]{:S(2)}) async-start(bf16[128,512,128]{2,0,1:T(8,128)(2,1)} %all-gather.2.cloned.1.call-done), calls=%async_computation | async-start | bytes 33554432 | tf_op jit(solution)/shard_map/all_to_all | solution.py:55
  173.0 552.8 %copy-start.13 = (bf16[128,128]{1,0:T(8,128)(2,1)S(1)}, bf16[128,128]{1,0:T(8,128)(2,1)}, u32[]{:S(2)}) copy-start(bf16[128,128]{1,0:T(8,128)(2,1)} %param.14) | copy-start | bytes 98308
  173.0 360.5 %collective-permute-start = (bf16[128,128,128]{0,2,1:T(8,128)(2,1)}, bf16[128,128,128]{0,2,1:T(8,128)(2,1)S(1)}, u32[]{:S(2)}, u32[]{:S(2)}) collective-permute-start(bf16[128,128,128]{0,2,1:T(8,128)(2,1)} %get-tuple-element.6), channel_id=1, source_target_pairs={{0,12},{4,0},{8,4},{12,8},{1,13},{5,1},{9,5},{13,9},{2,14},{6,2},{... | collective-permute-start | bytes 12582920 | tf_op jit(solution)/shard_map/ppermute | solution.py:14
  533.5 2.0 copy-start.7
  535.5 183.6 %collective-permute-start.1 = (bf16[128,128,128]{0,2,1:T(8,128)(2,1)S(1)}, bf16[128,128,128]{0,2,1:T(8,128)(2,1)}, u32[]{:S(2)}, u32[]{:S(2)}) collective-permute-start(bf16[128,128,128]{0,2,1:T(8,128)(2,1)S(1)} %collective-permute-done), channel_id=1, source_target_pairs={{0,12},{4,0},{8,4},{12,8},{1,13},{5,1},{9,5},{13,9},{2,14},{6,2},{... | collective-permute-start | bytes 12582920 | tf_op jit(solution)/shard_map/ppermute | solution.py:14
  719.1 91.6 %collective-permute-start.2 = (bf16[128,128,128]{0,2,1:T(8,128)(2,1)}, bf16[128,128,128]{0,2,1:T(8,128)(2,1)}, u32[]{:S(2)}, u32[]{:S(2)}) collective-permute-start(bf16[128,128,128]{0,2,1:T(8,128)(2,1)} %collective-permute-done.1), channel_id=1, source_target_pairs={{0,12},{4,0},{8,4},{12,8},{1,13},{5,1},{9,5},{13,9},{2,14},{6,2},{... | collective-permute-start | bytes 12582920 | tf_op jit(solution)/shard_map/ppermute | solution.py:14
  864.3 10.1 %copy-start.3 = (bf16[128,128,512]{2,1,0:T(8,128)(2,1)S(1)}, bf16[128,128,512]{2,1,0:T(8,128)(2,1)}, u32[]{:S(2)}) copy-start(bf16[128,128,512]{2,1,0:T(8,128)(2,1)} %all_to_all.16) | copy-start | bytes 50331652
  874.5 8.6 copy-start.6
  906.2 5.8 copy-start.2
  906.2 5.8 copy-start.11
  906.2 5.8 copy-start.12
  910.7 3.4 copy-start.8
  914.0 14.4 %copy-start.1 = (bf16[128,512]{1,0:T(8,128)(2,1)S(1)}, bf16[128,512]{1,0:T(8,128)(2,1)}, u32[]{:S(2)}) copy-start(bf16[128,512]{1,0:T(8,128)(2,1)} %param.13) | copy-start | bytes 393220
Sparse Core Ops, SparseCore 0:
  57.4 108.6 all-gather.1
